TPU v7x, 32 devices: a whole 2x2x4 slice. The times are simulated.
32 devices in a mesh: groups: 2 (over x), cent: 16 (over z, y, core).
Axes of the slice: x: 2, y: 2, z: 4, core: 2. Of those that a mesh axis runs over, the one named last changes fastest.
Arguments:
- points: bfloat16 [1024, 768], P(('groups', 'cent')), parts along dimension 0, may hold values from -64 to 64, as said below
- centroids: bfloat16 [131072, 768], P(('groups', 'cent')), parts along dimension 0, may hold values from -1 to 1
- coarse_init: float32 [4096, 768], P(('groups', 'cent')), parts along dimension 0, may hold values from -2.4 to 2.4
- assign: int32 [131072], P(('groups', 'cent')), parts along dimension 0, may hold values from 0 to 2047, as said below
Outputs:
- level_one: bfloat16 [131072, 768], P(('groups', 'cent')), parts along dimension 0
- level_two: float32 [4096, 768], P(('groups', 'cent')), parts along dimension 0
There are 2 independent parts, one for each index of `groups`. A program takes and returns all parts, laid end to end along the dimension named above; each array names one. Nothing has to cross between parts.
Inputs may be any that keep to these rules, and one draw needn't show every extreme that they name: `points`: entries normal (clipped at 8) or uniform within 1.7; on some draws a few rows are scaled multiples of a centroid that has a close twin, giving logits up to about 300. `assign`: among the 65536 // 16 level-1 centroids held by one index of cent, at most 512 have their level-2 centroid in any one block of 2048 // 16 consecutive level-2 centroids, and some block receives exactly 512.
All inputs are finite; a program needn't handle non-finite values.
Results may differ from a plain program's by a relative error of at most 0.0039.
Values may be sent and summed in bfloat16 or wider, within the bound.
A program may use at most 64 MiB of HBM per device.

v0:
```python
import math
import jax
import jax.numpy as jnp
from jax import lax
from jax.sharding import PartitionSpec as P

D = 768
K2 = 2048
TEMP = 0.05
PRIOR_ONE = 0.02
PRIOR_TWO = 0.25


def shards(points, centroids, coarse_init, assign):
    scale = 1.0 / (TEMP * math.sqrt(D))
    everyone = lax.all_gather(points, "cent", axis=0, tiled=True)
    count = everyone.shape[0]
    rows = min(512, count)
    pblocks = everyone.reshape(count // rows, rows, D)
    local_k = centroids.shape[0]

    def logits_of(block):
        return (
            lax.dot_general(
                block, centroids, (((1,), (1,)), ((), ())), preferred_element_type=jnp.float32
            )
            * scale
        )

    def local_stats(block):
        logits = logits_of(block)
        top = jnp.max(logits, axis=1)
        return (top, jnp.sum(jnp.exp(logits - top[:, None]), axis=1))

    local_top, local_sum = lax.map(local_stats, pblocks)
    local_top = local_top.reshape(count)
    local_sum = local_sum.reshape(count)
    peak = lax.pmax(local_top, "cent")
    total = lax.psum(local_sum * jnp.exp(local_top - peak), "cent")
    peaks = peak.reshape(count // rows, rows)
    totals = total.reshape(count // rows, rows)

    def accumulate(carry, item):
        block, peak_rows, total_rows = item
        resp = jnp.exp(logits_of(block) - peak_rows[:, None]) / total_rows[:, None]
        mass = carry[0] + jnp.sum(resp, axis=0)
        weighted = carry[1] + lax.dot_general(
            resp.astype(jnp.bfloat16),
            block,
            (((0,), (0,)), ((), ())),
            preferred_element_type=jnp.float32,
        )
        return ((mass, weighted), None)

    start_carry = (jnp.zeros((local_k,), jnp.float32), jnp.zeros((local_k, D), jnp.float32))
    (mass, weighted), _ = lax.scan(accumulate, start_carry, (pblocks, peaks, totals))
    fresh = (weighted + PRIOR_ONE * centroids.astype(jnp.float32)) / (mass[:, None] + PRIOR_ONE)
    level_one = fresh.astype(jnp.bfloat16)
    moved = (mass[:, None] * fresh).astype(jnp.bfloat16)
    mass_high = mass.astype(jnp.bfloat16)
    mass_low = (mass - mass_high.astype(jnp.float32)).astype(jnp.bfloat16)
    onehot = (assign[:, None] == lax.broadcasted_iota(jnp.int32, (1, K2), 1)).astype(jnp.bfloat16)
    wsum_term = lax.dot_general(
        onehot, moved, (((0,), (0,)), ((), ())), preferred_element_type=jnp.float32
    )
    mass_pair = jnp.stack([mass_high, mass_low])
    msum_term = jnp.sum(jnp.dot(mass_pair, onehot, preferred_element_type=jnp.float32), axis=0)
    wsum, msum = (
        lax.psum_scatter(wsum_term, "cent", scatter_dimension=0, tiled=True),
        lax.psum_scatter(msum_term, "cent", scatter_dimension=0, tiled=True),
    )
    level_two = (wsum + PRIOR_TWO * coarse_init) / (msum[:, None] + PRIOR_TWO)
    return (level_one, level_two)


def solution(mesh):
    return jax.shard_map(
        shards,
        mesh=mesh,
        in_specs=(
            P(("groups", "cent"), None),
            P(("groups", "cent"), None),
            P(("groups", "cent"), None),
            P(("groups", "cent")),
        ),
        out_specs=(P(("groups", "cent"), None), P(("groups", "cent"), None)),
        check_vma=False,
    )
```

profile of v0, /device:TPU:0, one launch (start us, length us, event | category | flops | bytes accessed | tf_op | source)
XLA Modules:
  0.0 236.3 jit_solution(16250268285683801577)
XLA Ops:
  7.2 0.0 reduce-scatter.2.cloned.1.call-start
  7.2 25.7 %all_gather.3 = bf16[512,768]{1,0:T(8,128)(2,1)S(1)} all-gather(bf16[32,768]{1,0:T(8,128)(2,1)} %param.4), channel_id=1, replica_groups=mesh['groups'=2,'cent'=16] {'cent'}, dimensions={0}, use_global_device_ids=true | all-gather | bytes 835584 | tf_op jit(solution)/shard_map/all_gather | solution.py:16
  32.9 8.4 %multiply_reduce_fusion = (f32[512]{0:T(512)S(1)}, f32[512,4096]{1,0:T(8,128)}) fusion(bf16[512,768]{1,0:T(8,128)(2,1)S(1)} %all_gather.3, bf16[4096,768]{1,0:T(8,128)(2,1)} %param.5), kind=kOutput, calls=%fused_computation.9 | convolution fusion | flops 3225419264 | bytes 15468544 | tf_op jit(solution)/shard_map/while/body/eval_jaxpr/dot_general | solution.py:24
  41.4 29.8 %pmax.7 = f32[512]{0:T(512)S(1)} all-reduce(f32[512]{0:T(512)S(1)} %get-tuple-element.24), channel_id=1, replica_groups=mesh['groups'=2,'cent'=16] {'cent'}, use_global_device_ids=true, to_apply=%region_1.0 | all-reduce | flops 512 | bytes 4096 | tf_op jit(solution)/shard_map/pmax | solution.py:38
  71.2 4.9 %exponential_reduce_fusion = f32[512]{0:T(512)S(1)} fusion(f32[512,4096]{1,0:T(8,128)} %get-tuple-element.25, f32[512]{0:T(512)S(1)} %get-tuple-element.24), kind=kLoop, calls=%fused_computation.7 | loop fusion | flops 6290944 | bytes 8392704 | tf_op jit(solution)/shard_map/while/body/eval_jaxpr/reduce_sum | solution.py:33
  76.1 29.5 %psum.7 = f32[512]{0:T(512)S(1)} all-reduce(f32[512]{0:T(512)S(1)} %exponential_multiply_fusion), channel_id=1, replica_groups=mesh['groups'=2,'cent'=16] {'cent'}, use_global_device_ids=true, to_apply=%region_3.4 | all-reduce | flops 512 | bytes 4096 | tf_op jit(solution)/shard_map/psum | solution.py:39
  105.6 4.5 %fusion.11 = f32[4096]{0:T(1024)S(1)} fusion(f32[512]{0:T(512)S(1)} %psum.7, f32[512]{0:T(512)S(1)} %pmax.7, f32[512,4096]{1,0:T(8,128)} %get-tuple-element.25), kind=kLoop, calls=%fused_computation.22 | loop fusion | flops 8384512 | bytes 8409088 | tf_op jit(solution)/shard_map/while/body/eval_jaxpr/reduce_sum | solution.py:46
  110.1 0.0 copy-start.1
  110.1 12.1 %fusion.12 = (bf16[4096,768]{1,0:T(8,128)(2,1)}, f32[4096,768]{1,0:T(8,128)}) fusion(f32[4096]{0:T(1024)S(1)} %broadcast_add_fusion, bf16[4096,768]{1,0:T(8,128)(2,1)} %param.5, bf16[512,768]{1,0:T(8,128)(2,1)S(1)} %all_gather.3, f32[512]{0:T(512)S(1)} %psum.7, f32[512]{0:T(512)S(1)} %pmax.7, f32[512,4096]{1,0:T(8,128)} %get-tuple-element.25), kind=kOutput, calls=%fused_computation.23 | convolution fusion | flops 3245342720 | bytes 34361344 | tf_op jit(solution)/shard_map/while/body/eval_jaxpr/dot_general | solution.py:47
  122.1 0.0 copy-done.1
  122.1 0.0 copy-start.2
  122.1 22.7 %fusion.1 = f32[2048,768]{1,0:T(8,128)} fusion(s32[4096]{0:T(1024)S(1)} %copy-done.1, f32[4096,768]{1,0:T(8,128)} %get-tuple-element.34, f32[4096]{0:T(1024)S(1)} %fusion.11), kind=kOutput, calls=%fused_computation.2 | convolution fusion | flops 12899581952 | bytes 18907136 | tf_op jit(solution)/shard_map/dot_general | solution.py:63
  144.9 0.0 copy-start
  144.9 0.0 reduce-scatter.2.cloned.1.call-update
  144.9 0.0 copy-done.2
  145.0 0.6 dynamic-slice.3
  146.2 5.9 %fusion.6 = f32[2048]{0:T(1024)S(1)} fusion(s32[4096]{0:T(1024)S(1)} %copy-done.1, bf16[1,4096]{1,0:T(2,128)(2,1)S(1)} %subtract_convert_fusion, bf16[1,4096]{1,0:T(2,128)(2,1)S(1)} %convert_element_type.52), kind=kOutput, calls=%fused_computation.12 | convolution fusion | flops 41977856 | bytes 40960 | tf_op jit(solution)/shard_map/dot_general | solution.py:67
  152.1 30.7 %all-reduce = f32[2048]{0:T(1024)S(1)} all-reduce(f32[2048]{0:T(1024)S(1)} %fusion.6), channel_id=3, replica_groups=mesh['groups'=2,'cent'=16] {'cent'}, use_global_device_ids=true, to_apply=%region_7.8.clone | all-reduce | flops 2048 | bytes 16384
  182.8 0.1 dynamic-slice_add_fusion
  182.9 44.7 %reduce-scatter.2.cloned.1.call-done = f32[128,768]{1,0:T(8,128)} async-done(((f32[2048,768]{1,0:T(8,128)}), f32[128,768]{1,0:T(8,128)}) %reduce-scatter.2.cloned.1.call-update) | async-done | bytes 393232 | tf_op jit(solution)/shard_map/reduce_scatter | solution.py:69
  227.6 0.0 copy-done
  227.6 1.8 add_divide_fusion.1
  (4 shorter events, 0.0 us)
Async XLA Ops:
  7.2 220.5 %reduce-scatter.2.cloned.1.call-start = ((), (), s32[]{:S(2)}) async-start(), calls=%async_computation.1 | async-start | bytes 6684672 | tf_op jit(solution)/shard_map/reduce_scatter | solution.py:69
  110.1 12.1 %copy-start.1 = (s32[4096]{0:T(1024)S(1)}, s32[4096]{0:T(1024)}, u32[]{:S(2)}) copy-start(s32[4096]{0:T(1024)} %param.7) | copy-start | bytes 49156
  122.1 22.8 %copy-start.2 = (u32[32]{0:T(128)S(1)}, u32[32]{0:T(128)}, u32[]{:S(2)}) copy-start(u32[32]{0:T(128)} %constant.43) | copy-start | bytes 388
  144.9 82.8 %copy-start = (f32[128,768]{1,0:T(8,128)S(1)}, f32[128,768]{1,0:T(8,128)}, u32[]{:S(2)}) copy-start(f32[128,768]{1,0:T(8,128)} %param.6) | copy-start | bytes 1179652
Sparse Core Ops, SparseCore 0:
  145.0 82.5 reduce-scatter.1
where the time goes:
time: 237 us; the launch traced here: 236 us
  blocking collectives  116 us (49%)
  matrix products  49.1 us (21%)
  waiting for transfers between devices  44.8 us (19%)
  between operations  14.8 us (6%)
  other arithmetic  11.3 us (5%)
    reduce_scatter x1, waiting for transfers between devices, shards(): lax.psum_scatter(wsum_term, 'cent', scatter_dimension=0, tiled=True)  44.7 us
    unnamed x1, blocking collectives  30.7 us
    pmax x1, blocking collectives, shards(): peak = lax.pmax(local_top, 'cent')  29.8 us
    psum x1, blocking collectives, shards(): total = lax.psum(local_sum * jnp.exp(local_top - peak), 'cent')  29.5 us
    all_gather x1, blocking collectives, shards(): everyone = lax.all_gather(points, 'cent', axis=0, tiled=True)  25.7 us
    dot_general x1, matrix products, shards(): lax.dot_general(onehot, moved, (((0,), (0,)), ((), ())), preferred_elemen...  22.7 us
    dot_general x1, matrix products, accumulate(): lax.dot_general(resp.astype(jnp.bfloat16), block, (((0,), (0,)), ((), ())...  12.1 us
    dot_general x1, matrix products, logits_of(): lax.dot_general(block, centroids, (((1,), (1,)), ((), ())), preferred_ele...  8.45 us
  transfers between devices with their start and end apart: 1, of which 1 were waited for; matrix products, arithmetic and copies ran while one was open for 3% of the time, Pallas kernels for 0%

commit v1 on v0

--- a/solution.py
+++ b/solution.py
@@ -36,7 +36,7 @@
     local_top = local_top.reshape(count)
     local_sum = local_sum.reshape(count)
     peak = lax.pmax(local_top, "cent")
-    total = lax.psum(local_sum * jnp.exp(local_top - peak), "cent")
+    total = jnp.sum(lax.all_gather(local_sum * jnp.exp(local_top - peak), "cent"), axis=0)
     peaks = peak.reshape(count // rows, rows)
     totals = total.reshape(count // rows, rows)
 

time: 237 us -> 226 us (0.954)
  blocking collectives: 116 us -> 106 us
    psum x1 -> x0, blocking collectives: 29.5 us -> none  [shards(): total = lax.psum(local_sum * jnp.exp(local_top - peak), 'cent')]
    all_gather x0 -> x1, blocking collectives: none -> 17.2 us  [shards(): lax.all_gather(local_sum * jnp.exp(local_top - peak), 'cent')]
where the time goes in v1:
time: 226 us; the launch traced here: 225 us
  blocking collectives  106 us (47%)
  matrix products  49.1 us (22%)
  waiting for transfers between devices  44 us (19%)
  between operations  14.8 us (7%)
  other arithmetic  11.3 us (5%)
    reduce_scatter x1, waiting for transfers between devices, shards(): lax.psum_scatter(wsum_term, 'cent', scatter_dimension=0, tiled=True)  43.9 us
    unnamed x1, blocking collectives  32.9 us
    pmax x1, blocking collectives, shards(): peak = lax.pmax(local_top, 'cent')  29.8 us
    all_gather x1, blocking collectives, shards(): everyone = lax.all_gather(points, 'cent', axis=0, tiled=True)  25.7 us
    dot_general x1, matrix products, shards(): lax.dot_general(onehot, moved, (((0,), (0,)), ((), ())), preferred_elemen...  22.7 us
    all_gather x1, blocking collectives, shards(): lax.all_gather(local_sum * jnp.exp(local_top - peak), 'cent')  17.2 us
    dot_general x1, matrix products, accumulate(): lax.dot_general(resp.astype(jnp.bfloat16), block, (((0,), (0,)), ((), ())...  12.1 us
    dot_general x1, matrix products, logits_of(): lax.dot_general(block, centroids, (((1,), (1,)), ((), ())), preferred_ele...  8.45 us
  transfers between devices with their start and end apart: 1, of which 1 were waited for; matrix products, arithmetic and copies ran while one was open for 3% of the time, Pallas kernels for 0%

profile of v1, /device:TPU:0, one launch (start us, length us, event | category | flops | bytes accessed | tf_op | source)
XLA Modules:
  0.0 225.5 jit_solution(10477984378221761078)
XLA Ops:
  7.2 0.0 reduce-scatter.2.cloned.1.call-start
  7.2 25.7 %all_gather.9 = bf16[512,768]{1,0:T(8,128)(2,1)S(1)} all-gather(bf16[32,768]{1,0:T(8,128)(2,1)} %param.4), channel_id=1, replica_groups=mesh['groups'=2,'cent'=16] {'cent'}, dimensions={0}, use_global_device_ids=true | all-gather | bytes 835584 | tf_op jit(solution)/shard_map/all_gather | solution.py:16
  32.9 8.4 %multiply_reduce_fusion = (f32[512]{0:T(512)S(1)}, f32[512,4096]{1,0:T(8,128)}) fusion(bf16[512,768]{1,0:T(8,128)(2,1)S(1)} %all_gather.9, bf16[4096,768]{1,0:T(8,128)(2,1)} %param.5), kind=kOutput, calls=%fused_computation.9 | convolution fusion | flops 3225419264 | bytes 15468544 | tf_op jit(solution)/shard_map/while/body/eval_jaxpr/dot_general | solution.py:24
  41.4 29.8 %pmax.7 = f32[512]{0:T(512)S(1)} all-reduce(f32[512]{0:T(512)S(1)} %get-tuple-element.24), channel_id=1, replica_groups=mesh['groups'=2,'cent'=16] {'cent'}, use_global_device_ids=true, to_apply=%region_1.0 | all-reduce | flops 512 | bytes 4096 | tf_op jit(solution)/shard_map/pmax | solution.py:38
  71.2 4.9 %exponential_reduce_fusion = f32[512]{0:T(512)S(1)} fusion(f32[512,4096]{1,0:T(8,128)} %get-tuple-element.25, f32[512]{0:T(512)S(1)} %get-tuple-element.24), kind=kLoop, calls=%fused_computation.7 | loop fusion | flops 6290944 | bytes 8392704 | tf_op jit(solution)/shard_map/while/body/eval_jaxpr/reduce_sum | solution.py:33
  76.1 17.2 %all-gather.1 = f32[16,1,512]{2,1,0:T(1,128)S(1)} all-gather(f32[1,1,512]{2,1,0:T(1,128)S(1)} %bitcast.8), channel_id=2, replica_groups=mesh['groups'=2,'cent'=16] {'cent'}, dimensions={0}, use_global_device_ids=true | all-gather | bytes 34816 | tf_op jit(solution)/shard_map/all_gather | solution.py:39
  93.3 4.5 %fusion.11 = f32[4096]{0:T(1024)S(1)} fusion(f32[512]{0:T(512)S(1)} %reduce_sum.41, f32[512]{0:T(512)S(1)} %pmax.7, f32[512,4096]{1,0:T(8,128)} %get-tuple-element.25), kind=kLoop, calls=%fused_computation.22 | loop fusion | flops 8384512 | bytes 8409088 | tf_op jit(solution)/shard_map/while/body/eval_jaxpr/reduce_sum | solution.py:46
  97.8 0.0 copy-start.1
  97.8 12.1 %fusion.12 = (bf16[4096,768]{1,0:T(8,128)(2,1)}, f32[4096,768]{1,0:T(8,128)}) fusion(f32[4096]{0:T(1024)S(1)} %broadcast_add_fusion, bf16[4096,768]{1,0:T(8,128)(2,1)} %param.5, bf16[512,768]{1,0:T(8,128)(2,1)S(1)} %all_gather.9, f32[512]{0:T(512)S(1)} %reduce_sum.41, f32[512]{0:T(512)S(1)} %pmax.7, f32[512,4096]{1,0:T(8,128)} %get-tuple-element.25), kind=kOutput, calls=%fused_computation.23 | convolution fusion | flops 3245342720 | bytes 34361344 | tf_op jit(solution)/shard_map/while/body/eval_jaxpr/dot_general | solution.py:47
  109.9 0.0 copy-done.1
  109.9 0.0 copy-start.2
  109.9 22.7 %fusion.1 = f32[2048,768]{1,0:T(8,128)} fusion(s32[4096]{0:T(1024)S(1)} %copy-done.1, f32[4096,768]{1,0:T(8,128)} %get-tuple-element.34, f32[4096]{0:T(1024)S(1)} %fusion.11), kind=kOutput, calls=%fused_computation.2 | convolution fusion | flops 12899581952 | bytes 18907136 | tf_op jit(solution)/shard_map/dot_general | solution.py:63
  132.6 0.0 copy-start
  132.6 0.0 reduce-scatter.2.cloned.1.call-update
  132.7 0.0 copy-done.2
  132.7 0.6 dynamic-slice.3
  134.0 5.9 %fusion.6 = f32[2048]{0:T(1024)S(1)} fusion(s32[4096]{0:T(1024)S(1)} %copy-done.1, bf16[1,4096]{1,0:T(2,128)(2,1)S(1)} %subtract_convert_fusion, bf16[1,4096]{1,0:T(2,128)(2,1)S(1)} %convert_element_type.52), kind=kOutput, calls=%fused_computation.12 | convolution fusion | flops 41977856 | bytes 40960 | tf_op jit(solution)/shard_map/dot_general | solution.py:67
  139.8 32.9 %all-reduce = f32[2048]{0:T(1024)S(1)} all-reduce(f32[2048]{0:T(1024)S(1)} %fusion.6), channel_id=4, replica_groups=mesh['groups'=2,'cent'=16] {'cent'}, use_global_device_ids=true, to_apply=%region_7.8.clone | all-reduce | flops 2048 | bytes 16384
  172.7 0.1 dynamic-slice_add_fusion
  172.8 43.9 %reduce-scatter.2.cloned.1.call-done = f32[128,768]{1,0:T(8,128)} async-done(((f32[2048,768]{1,0:T(8,128)}), f32[128,768]{1,0:T(8,128)}) %reduce-scatter.2.cloned.1.call-update) | async-done | bytes 393232 | tf_op jit(solution)/shard_map/reduce_scatter | solution.py:69
  216.8 0.0 copy-done
  216.8 1.8 add_divide_fusion.1
  (5 shorter events, 0.1 us)
Async XLA Ops:
  7.2 209.6 %reduce-scatter.2.cloned.1.call-start = ((), (), s32[]{:S(2)}) async-start(), calls=%async_computation.1 | async-start | bytes 6684672 | tf_op jit(solution)/shard_map/reduce_scatter | solution.py:69
  97.8 12.1 %copy-start.1 = (s32[4096]{0:T(1024)S(1)}, s32[4096]{0:T(1024)}, u32[]{:S(2)}) copy-start(s32[4096]{0:T(1024)} %param.7) | copy-start | bytes 49156
  109.9 22.8 %copy-start.2 = (u32[32]{0:T(128)S(1)}, u32[32]{0:T(128)}, u32[]{:S(2)}) copy-start(u32[32]{0:T(128)} %constant.43) | copy-start | bytes 388
  132.6 84.1 %copy-start = (f32[128,768]{1,0:T(8,128)S(1)}, f32[128,768]{1,0:T(8,128)}, u32[]{:S(2)}) copy-start(f32[128,768]{1,0:T(8,128)} %param.6) | copy-start | bytes 1179652
Sparse Core Ops, SparseCore 0:
  132.8 83.9 reduce-scatter.1
